TPU v7x, 256 devices: a 8x8x2 block of a 8x8x16 slice. The times are simulated.
256 devices in a mesh: parts: 2 (over z), uly: 8 (over x), blk: 16 (over y, core).
Axes of the slice: x: 8, y: 8, z: 2, core: 2. Of those that a mesh axis runs over, the one named last changes fastest.
The devices are a block of a 8x8x16 slice.
Arguments:
- queries: bfloat16 [32, 512, 8192], P(('parts', 'blk'), 'uly'), parts along dimension 0, may hold values from -4.5 to 4.5
- keys: bfloat16 [32, 512, 1024], P(('parts', 'blk'), 'uly'), parts along dimension 0, may hold values from -4.5 to 4.5
- values: bfloat16 [32, 512, 1024], P(('parts', 'blk'), 'uly'), parts along dimension 0, may hold values from -6 to 6
- doc_blocks: int32 [32], P('parts'), parts along dimension 0, may hold values from 1 to 36, 64 in all
Outputs:
- attended: bfloat16 [32, 512, 8192], P(('parts', 'blk'), 'uly'), parts along dimension 0
There are 2 independent parts, one for each index of `parts`. A program takes and returns all parts, laid end to end along the dimension named above; each array names one. Nothing has to cross between parts.
Inputs may be any that keep to these rules, and one draw needn't show every extreme that they name: `doc_blocks`: the lengths sum to 64; the longest document holds exactly (9) * 512 tokens.
All inputs are finite; a program needn't handle non-finite values.
Results may differ from a plain program's by a relative error of at most 0.0037.
Values may be sent and summed in bfloat16 or wider, within the bound.
No kernel may reach another device: no remote copies, remote signals or barrier semaphores. Data moves between devices by JAX's collectives and lax.ppermute only.
A program may use at most 128 MiB of HBM per device.

v0:
```python
import jax
import jax.numpy as jnp
from jax import lax
from jax.sharding import PartitionSpec as P

HEAD_WIDTH = 128
BLOCK = 128


def side_by_side(arrays, axis, split_dim, concat_dim, along):
    ends, at = ([], 0)
    for a in arrays[:-1]:
        at += a.shape[along]
        ends.append(at)
    both = jnp.concatenate(arrays, axis=along)
    return tuple(
        jnp.split(
            lax.all_to_all(both, axis, split_axis=split_dim, concat_axis=concat_dim, tiled=True),
            ends,
            axis=along,
        )
    )


def segment_of(positions, ends):
    return jnp.sum((positions[:, None] >= ends[None, :]).astype(jnp.int32), axis=1)


def on_device(queries, keys, values, doc_blocks):
    moved_q, moved_k, moved_v = (
        lax.all_to_all(queries, "uly", split_axis=2, concat_axis=1, tiled=True),
        *side_by_side((keys, values), "uly", 2, 1, 0),
    )
    slot = moved_q.shape[1]
    local_q = moved_q.shape[2] // HEAD_WIDTH
    local_kv = moved_k.shape[2] // HEAD_WIDTH
    query_group = local_q // local_kv
    scale = HEAD_WIDTH ** (-0.5)
    first_index = lax.axis_index("blk") * slot
    ends = jnp.cumsum(doc_blocks) * BLOCK
    qpos = first_index + jnp.arange(slot, dtype=jnp.int32)
    qseg = segment_of(qpos, ends)
    qheads = jnp.transpose(moved_q[0].reshape(slot, local_q, HEAD_WIDTH), (1, 0, 2))
    stacked = jnp.concatenate([moved_k, moved_v], axis=0)

    def allowed_for(kpos):
        kseg = segment_of(kpos, ends)
        return (qseg[:, None] == kseg[None, :]) & (kpos[None, :] <= qpos[:, None])

    start_state = (
        jnp.full((local_q, slot), -1e30, jnp.float32),
        jnp.zeros((local_q, slot), jnp.float32),
        jnp.zeros((local_q, slot, HEAD_WIDTH), jnp.float32),
    )
    piece = lax.all_gather(stacked, "blk", axis=1, tiled=True)
    start = jnp.int32(0)
    count = piece.shape[1]

    def work(state):
        key_piece = piece[0].reshape(count, local_kv, HEAD_WIDTH)
        value_piece = piece[1].reshape(count, local_kv, HEAD_WIDTH)
        allowed = allowed_for(jnp.arange(count, dtype=jnp.int32))

        def one_head(inputs):
            head, running, summed, accum = inputs
            qh = lax.dynamic_index_in_dim(qheads, head, 0, keepdims=False)
            kh = lax.dynamic_index_in_dim(key_piece, head // query_group, 1, keepdims=False)
            vh = lax.dynamic_index_in_dim(value_piece, head // query_group, 1, keepdims=False)
            scores = jnp.dot(qh, kh.T, preferred_element_type=jnp.float32) * scale
            scores = jnp.where(allowed, scores, -1e30)
            newest = jnp.maximum(running, jnp.max(scores, axis=1))
            expo = jnp.where(allowed, jnp.exp(scores - newest[:, None]), 0.0)
            factor = jnp.exp(running - newest)
            summed = summed * factor + jnp.sum(expo, axis=1)
            accum = accum * factor[:, None] + jnp.dot(
                expo.astype(jnp.bfloat16), vh, preferred_element_type=jnp.float32
            )
            return (newest, summed, accum)

        return lax.map(one_head, (jnp.arange(local_q, dtype=jnp.int32),) + tuple(state))

    last_seg = jnp.sum((start + count - 1 >= ends).astype(jnp.int32))
    useful = (start < first_index + slot) & (last_seg >= qseg[0])
    running, summed, accum = lax.cond(useful, work, lambda state: state, start_state)
    heads = (accum / summed[:, :, None]).astype(jnp.bfloat16)
    outputs = jnp.transpose(heads, (1, 0, 2)).reshape(1, slot, local_q * HEAD_WIDTH)
    return lax.all_to_all(outputs, "uly", split_axis=1, concat_axis=2, tiled=True)


def solution(mesh):
    return jax.shard_map(
        on_device,
        mesh=mesh,
        in_specs=(
            P(("parts", "blk"), "uly", None),
            P(("parts", "blk"), "uly", None),
            P(("parts", "blk"), "uly", None),
            P("parts"),
        ),
        out_specs=P(("parts", "blk"), "uly", None),
        check_vma=False,
    )
```

profile of v0, /device:TPU:720, one launch (start us, length us, event | category | flops | bytes accessed | tf_op | source)
XLA Modules:
  0.0 406.6 jit_solution(11912159211561026626)
XLA Ops:
  8.3 19.1 %all_to_all.48 = bf16[8,2,8192]{2,1,0:T(2,128)(2,1)S(1)} all-to-all(bf16[8,2,8192]{2,1,0:T(2,128)(2,1)S(1)} %reshape.78), channel_id=1, replica_groups=mesh['parts'=2,'uly'=8,'blk'=16] {'uly'}, dimensions={0} | all-to-all | bytes 524288 | tf_op jit(solution)/shard_map/all_to_all | solution.py:18
  30.2 9.2 %copy.58 = bf16[1,64,8192]{1,0,2:T(2,128)(2,1)} copy(bf16[1,64,8192]{2,1,0:T(8,128)(2,1)} %param.8) | data formatting | bytes 2097152 | tf_op args[0]
  39.9 45.1 %reduce.2 = bf16[8192,64]{1,0:T(8,128)(2,1)S(1)} reduce(bf16[8192,1,64]{2,1,0:T(2,128)(2,1)} %bitcast.72, bf16[]{:T(256)} %broadcast.102), dimensions={1}, to_apply=%bitcast.51.reduce_sub_computation | reduce | bytes 2097154
  94.2 24.5 %all-to-all-done.1 = bf16[8,2,32768]{2,1,0:T(2,128)(2,1)S(1)} async-done(((bf16[8,2,32768]{2,1,0:T(2,128)(2,1)}), bf16[8,2,32768]{2,1,0:T(2,128)(2,1)S(1)}, u32[]{:S(2)}, u32[]{:S(2)}) %all-to-all-start.1) | async-done | bytes 1048608 | tf_op jit(solution)/shard_map/all_to_all | solution.py:31
  123.1 8.2 %copy.59 = bf16[1,64,8192]{2,1,0:T(8,128)(2,1)S(1)} copy(bf16[1,64,8192]{1,0,2:T(2,128)(2,1)} %bitcast.73) | data formatting | bytes 2097152 | tf_op jit(solution)/shard_map/all_to_all | solution.py:31
  132.8 221.4 %conditional.1 = (f32[8,512]{1,0:T(8,128)}, f32[8,512,128]{1,2,0:T(8,128)}) conditional(s32[]{:T(128)} %convert_element_type.20, () %tuple.17, (bf16[2,8192,128]{2,1,0:T(8,128)(2,1)}, s32[512]{0:T(512)S(1)}, s32[16]{0:T(128)S(1)}, s32[]{:T(128)}, s32[512]{0:T(512)S(1)}, /*index=5*/bf16[8,512,128]{2,0,1:T(8,128)(2,1)S(1)}) %tuple.53), branch_computations={%region_3.4_spmd, %region_4.10_spmd} | conditional | flops 2240210944 | bytes 133736896 | solution.py:84
  138.2 216.0 %while.12 = (s32[]{:T(128)}, f32[8,512]{1,0:T(8,128)}, f32[8,512,128]{1,2,0:T(8,128)}, s32[8]{0:T(128)S(1)}, bf16[8,512,128]{2,1,0:T(8,128)(2,1)}, /*index=5*/bf...) while((s32[]{:T(128)}, f32[8,512]{1,0:T(8,128)}, ...), condition=%wide.region_9.9_spmd.clone, body=%wide.region_6.8_spmd.clone.sunk | while | flops 2239825408 | bytes 123214048 | solution.py:80
  141.0 6.8 %fusion.37 = (f32[512]{0:T(512)S(1)}, f32[512,8192]{1,0:T(8,128)S(1)}) fusion(s32[512]{0:T(512)S(1)} %get-tuple-element.266, s32[8192]{0:T(1024)S(1)} %get-tuple-element.264, s32[512]{0:T(512)S(1)} %get-tuple-element.265, bf16[8192,1,128]{2,0,1:T(8,128)(2,1)} %get-tuple-element.262, bf16[8,512,128]{2,1,0:T(8,128)(2,1)} %get-tuple-element.261, ...), kind=kOutput, calls=%fused_computation.5.clone.1 | convolution fusion | flops 1098907136 | bytes 19044356 | tf_op jit(solution)/shard_map/cond/branch_1_fun/while/body/eval_jaxpr/dot_general | solution.py:69
  155.3 9.1 %fusion.39 = f32[1,512,128]{2,1,0:T(8,128)S(1)} fusion(bf16[8192,1,128]{2,0,1:T(8,128)(2,1)S(1)} %get-tuple-element.263, f32[512,8192]{1,0:T(8,128)} %copy-done, s32[512]{0:T(512)S(1)} %get-tuple-element.266, s32[8192]{0:T(1024)S(1)} %get-tuple-element.264, f32[512]{0:T(512)S(1)} %broadcast_maximum_fusion.2, s32[512]{0:T(512)S(1)} %get-tuple-element.265, ...), kind=kOutput, calls=%fused_computation.13.clone.1 | convolution fusion | flops 1107361792 | bytes 19177472 | tf_op jit(solution)/shard_map/cond/branch_1_fun/while/body/eval_jaxpr/dot_general | solution.py:75
  168.0 6.8 %fusion.37 = (f32[512]{0:T(512)S(1)}, f32[512,8192]{1,0:T(8,128)S(1)}) fusion(s32[512]{0:T(512)S(1)} %get-tuple-element.266, s32[8192]{0:T(1024)S(1)} %get-tuple-element.264, s32[512]{0:T(512)S(1)} %get-tuple-element.265, bf16[8192,1,128]{2,0,1:T(8,128)(2,1)} %get-tuple-element.262, bf16[8,512,128]{2,1,0:T(8,128)(2,1)} %get-tuple-element.261, ...), kind=kOutput, calls=%fused_computation.5.clone.1 | convolution fusion | flops 1098907136 | bytes 19044356 | tf_op jit(solution)/shard_map/cond/branch_1_fun/while/body/eval_jaxpr/dot_general | solution.py:69
  182.3 9.1 %fusion.39 = f32[1,512,128]{2,1,0:T(8,128)S(1)} fusion(bf16[8192,1,128]{2,0,1:T(8,128)(2,1)S(1)} %get-tuple-element.263, f32[512,8192]{1,0:T(8,128)} %copy-done, s32[512]{0:T(512)S(1)} %get-tuple-element.266, s32[8192]{0:T(1024)S(1)} %get-tuple-element.264, f32[512]{0:T(512)S(1)} %broadcast_maximum_fusion.2, s32[512]{0:T(512)S(1)} %get-tuple-element.265, ...), kind=kOutput, calls=%fused_computation.13.clone.1 | convolution fusion | flops 1107361792 | bytes 19177472 | tf_op jit(solution)/shard_map/cond/branch_1_fun/while/body/eval_jaxpr/dot_general | solution.py:75
  194.9 6.8 %fusion.37 = (f32[512]{0:T(512)S(1)}, f32[512,8192]{1,0:T(8,128)S(1)}) fusion(s32[512]{0:T(512)S(1)} %get-tuple-element.266, s32[8192]{0:T(1024)S(1)} %get-tuple-element.264, s32[512]{0:T(512)S(1)} %get-tuple-element.265, bf16[8192,1,128]{2,0,1:T(8,128)(2,1)} %get-tuple-element.262, bf16[8,512,128]{2,1,0:T(8,128)(2,1)} %get-tuple-element.261, ...), kind=kOutput, calls=%fused_computation.5.clone.1 | convolution fusion | flops 1098907136 | bytes 19044356 | tf_op jit(solution)/shard_map/cond/branch_1_fun/while/body/eval_jaxpr/dot_general | solution.py:69
  209.3 9.1 %fusion.39 = f32[1,512,128]{2,1,0:T(8,128)S(1)} fusion(bf16[8192,1,128]{2,0,1:T(8,128)(2,1)S(1)} %get-tuple-element.263, f32[512,8192]{1,0:T(8,128)} %copy-done, s32[512]{0:T(512)S(1)} %get-tuple-element.266, s32[8192]{0:T(1024)S(1)} %get-tuple-element.264, f32[512]{0:T(512)S(1)} %broadcast_maximum_fusion.2, s32[512]{0:T(512)S(1)} %get-tuple-element.265, ...), kind=kOutput, calls=%fused_computation.13.clone.1 | convolution fusion | flops 1107361792 | bytes 19177472 | tf_op jit(solution)/shard_map/cond/branch_1_fun/while/body/eval_jaxpr/dot_general | solution.py:75
  222.0 6.8 %fusion.37 = (f32[512]{0:T(512)S(1)}, f32[512,8192]{1,0:T(8,128)S(1)}) fusion(s32[512]{0:T(512)S(1)} %get-tuple-element.266, s32[8192]{0:T(1024)S(1)} %get-tuple-element.264, s32[512]{0:T(512)S(1)} %get-tuple-element.265, bf16[8192,1,128]{2,0,1:T(8,128)(2,1)} %get-tuple-element.262, bf16[8,512,128]{2,1,0:T(8,128)(2,1)} %get-tuple-element.261, ...), kind=kOutput, calls=%fused_computation.5.clone.1 | convolution fusion | flops 1098907136 | bytes 19044356 | tf_op jit(solution)/shard_map/cond/branch_1_fun/while/body/eval_jaxpr/dot_general | solution.py:69
  236.3 9.1 %fusion.39 = f32[1,512,128]{2,1,0:T(8,128)S(1)} fusion(bf16[8192,1,128]{2,0,1:T(8,128)(2,1)S(1)} %get-tuple-element.263, f32[512,8192]{1,0:T(8,128)} %copy-done, s32[512]{0:T(512)S(1)} %get-tuple-element.266, s32[8192]{0:T(1024)S(1)} %get-tuple-element.264, f32[512]{0:T(512)S(1)} %broadcast_maximum_fusion.2, s32[512]{0:T(512)S(1)} %get-tuple-element.265, ...), kind=kOutput, calls=%fused_computation.13.clone.1 | convolution fusion | flops 1107361792 | bytes 19177472 | tf_op jit(solution)/shard_map/cond/branch_1_fun/while/body/eval_jaxpr/dot_general | solution.py:75
  249.0 6.8 %fusion.37 = (f32[512]{0:T(512)S(1)}, f32[512,8192]{1,0:T(8,128)S(1)}) fusion(s32[512]{0:T(512)S(1)} %get-tuple-element.266, s32[8192]{0:T(1024)S(1)} %get-tuple-element.264, s32[512]{0:T(512)S(1)} %get-tuple-element.265, bf16[8192,1,128]{2,0,1:T(8,128)(2,1)} %get-tuple-element.262, bf16[8,512,128]{2,1,0:T(8,128)(2,1)} %get-tuple-element.261, ...), kind=kOutput, calls=%fused_computation.5.clone.1 | convolution fusion | flops 1098907136 | bytes 19044356 | tf_op jit(solution)/shard_map/cond/branch_1_fun/while/body/eval_jaxpr/dot_general | solution.py:69
  263.3 9.1 %fusion.39 = f32[1,512,128]{2,1,0:T(8,128)S(1)} fusion(bf16[8192,1,128]{2,0,1:T(8,128)(2,1)S(1)} %get-tuple-element.263, f32[512,8192]{1,0:T(8,128)} %copy-done, s32[512]{0:T(512)S(1)} %get-tuple-element.266, s32[8192]{0:T(1024)S(1)} %get-tuple-element.264, f32[512]{0:T(512)S(1)} %broadcast_maximum_fusion.2, s32[512]{0:T(512)S(1)} %get-tuple-element.265, ...), kind=kOutput, calls=%fused_computation.13.clone.1 | convolution fusion | flops 1107361792 | bytes 19177472 | tf_op jit(solution)/shard_map/cond/branch_1_fun/while/body/eval_jaxpr/dot_general | solution.py:75
  276.0 6.8 %fusion.37 = (f32[512]{0:T(512)S(1)}, f32[512,8192]{1,0:T(8,128)S(1)}) fusion(s32[512]{0:T(512)S(1)} %get-tuple-element.266, s32[8192]{0:T(1024)S(1)} %get-tuple-element.264, s32[512]{0:T(512)S(1)} %get-tuple-element.265, bf16[8192,1,128]{2,0,1:T(8,128)(2,1)} %get-tuple-element.262, bf16[8,512,128]{2,1,0:T(8,128)(2,1)} %get-tuple-element.261, ...), kind=kOutput, calls=%fused_computation.5.clone.1 | convolution fusion | flops 1098907136 | bytes 19044356 | tf_op jit(solution)/shard_map/cond/branch_1_fun/while/body/eval_jaxpr/dot_general | solution.py:69
  290.3 9.1 %fusion.39 = f32[1,512,128]{2,1,0:T(8,128)S(1)} fusion(bf16[8192,1,128]{2,0,1:T(8,128)(2,1)S(1)} %get-tuple-element.263, f32[512,8192]{1,0:T(8,128)} %copy-done, s32[512]{0:T(512)S(1)} %get-tuple-element.266, s32[8192]{0:T(1024)S(1)} %get-tuple-element.264, f32[512]{0:T(512)S(1)} %broadcast_maximum_fusion.2, s32[512]{0:T(512)S(1)} %get-tuple-element.265, ...), kind=kOutput, calls=%fused_computation.13.clone.1 | convolution fusion | flops 1107361792 | bytes 19177472 | tf_op jit(solution)/shard_map/cond/branch_1_fun/while/body/eval_jaxpr/dot_general | solution.py:75
  302.9 6.8 %fusion.37 = (f32[512]{0:T(512)S(1)}, f32[512,8192]{1,0:T(8,128)S(1)}) fusion(s32[512]{0:T(512)S(1)} %get-tuple-element.266, s32[8192]{0:T(1024)S(1)} %get-tuple-element.264, s32[512]{0:T(512)S(1)} %get-tuple-element.265, bf16[8192,1,128]{2,0,1:T(8,128)(2,1)} %get-tuple-element.262, bf16[8,512,128]{2,1,0:T(8,128)(2,1)} %get-tuple-element.261, ...), kind=kOutput, calls=%fused_computation.5.clone.1 | convolution fusion | flops 1098907136 | bytes 19044356 | tf_op jit(solution)/shard_map/cond/branch_1_fun/while/body/eval_jaxpr/dot_general | solution.py:69
  317.3 9.1 %fusion.39 = f32[1,512,128]{2,1,0:T(8,128)S(1)} fusion(bf16[8192,1,128]{2,0,1:T(8,128)(2,1)S(1)} %get-tuple-element.263, f32[512,8192]{1,0:T(8,128)} %copy-done, s32[512]{0:T(512)S(1)} %get-tuple-element.266, s32[8192]{0:T(1024)S(1)} %get-tuple-element.264, f32[512]{0:T(512)S(1)} %broadcast_maximum_fusion.2, s32[512]{0:T(512)S(1)} %get-tuple-element.265, ...), kind=kOutput, calls=%fused_computation.13.clone.1 | convolution fusion | flops 1107361792 | bytes 19177472 | tf_op jit(solution)/shard_map/cond/branch_1_fun/while/body/eval_jaxpr/dot_general | solution.py:75
  329.9 6.8 %fusion.37 = (f32[512]{0:T(512)S(1)}, f32[512,8192]{1,0:T(8,128)S(1)}) fusion(s32[512]{0:T(512)S(1)} %get-tuple-element.266, s32[8192]{0:T(1024)S(1)} %get-tuple-element.264, s32[512]{0:T(512)S(1)} %get-tuple-element.265, bf16[8192,1,128]{2,0,1:T(8,128)(2,1)} %get-tuple-element.262, bf16[8,512,128]{2,1,0:T(8,128)(2,1)} %get-tuple-element.261, ...), kind=kOutput, calls=%fused_computation.5.clone.1 | convolution fusion | flops 1098907136 | bytes 19044356 | tf_op jit(solution)/shard_map/cond/branch_1_fun/while/body/eval_jaxpr/dot_general | solution.py:69
  344.3 9.1 %fusion.39 = f32[1,512,128]{2,1,0:T(8,128)S(1)} fusion(bf16[8192,1,128]{2,0,1:T(8,128)(2,1)S(1)} %get-tuple-element.263, f32[512,8192]{1,0:T(8,128)} %copy-done, s32[512]{0:T(512)S(1)} %get-tuple-element.266, s32[8192]{0:T(1024)S(1)} %get-tuple-element.264, f32[512]{0:T(512)S(1)} %broadcast_maximum_fusion.2, s32[512]{0:T(512)S(1)} %get-tuple-element.265, ...), kind=kOutput, calls=%fused_computation.13.clone.1 | convolution fusion | flops 1107361792 | bytes 19177472 | tf_op jit(solution)/shard_map/cond/branch_1_fun/while/body/eval_jaxpr/dot_general | solution.py:75
  365.6 31.7 %all_to_all.49 = bf16[8,2,32768]{2,1,0:T(2,128)(2,1)S(1)} all-to-all(bf16[8,2,32768]{2,1,0:T(2,128)(2,1)S(1)} %reshape.82), channel_id=1, replica_groups=mesh['parts'=2,'uly'=8,'blk'=16] {'uly'}, dimensions={0} | all-to-all | bytes 2097152 | tf_op jit(solution)/shard_map/all_to_all | solution.py:87
  (115 shorter events, 110.1 us)
Async XLA Ops:
  6.5 126.2 %all-gather.2.cloned.1.call-start = ((), (), s32[]{:S(2)}) async-start(), calls=%async_computation.3 | async-start | bytes 4456448 | tf_op jit(solution)/shard_map/all_gather | solution.py:55
  30.2 61.3 %copy-start.1 = (s32[16]{0:T(128)S(1)}, s32[16]{0:T(128)}, u32[]{:S(2)}) copy-start(s32[16]{0:T(128)} %param.11) | copy-start | bytes 196
  87.6 31.1 %all-to-all-start.1 = ((bf16[8,2,32768]{2,1,0:T(2,128)(2,1)}), bf16[8,2,32768]{2,1,0:T(2,128)(2,1)S(1)}, u32[]{:S(2)}, u32[]{:S(2)}) async-start(bf16[8,2,32768]{2,1,0:T(2,128)(2,1)} %reshape.80), calls=%async_computation.1 | async-start | bytes 2097152 | tf_op jit(solution)/shard_map/all_to_all | solution.py:31
  147.7 6.2 %copy-start = (f32[512,8192]{1,0:T(8,128)}, f32[512,8192]{1,0:T(8,128)S(1)}, u32[]{:S(2)}) copy-start(f32[512,8192]{1,0:T(8,128)S(1)} %get-tuple-element.228) | copy-start | bytes 50331652 | tf_op jit(solution)/shard_map/cond/branch_1_fun/while
  174.7 6.2 %copy-start = (f32[512,8192]{1,0:T(8,128)}, f32[512,8192]{1,0:T(8,128)S(1)}, u32[]{:S(2)}) copy-start(f32[512,8192]{1,0:T(8,128)S(1)} %get-tuple-element.228) | copy-start | bytes 50331652 | tf_op jit(solution)/shard_map/cond/branch_1_fun/while
  201.7 6.2 %copy-start = (f32[512,8192]{1,0:T(8,128)}, f32[512,8192]{1,0:T(8,128)S(1)}, u32[]{:S(2)}) copy-start(f32[512,8192]{1,0:T(8,128)S(1)} %get-tuple-element.228) | copy-start | bytes 50331652 | tf_op jit(solution)/shard_map/cond/branch_1_fun/while
  228.7 6.2 %copy-start = (f32[512,8192]{1,0:T(8,128)}, f32[512,8192]{1,0:T(8,128)S(1)}, u32[]{:S(2)}) copy-start(f32[512,8192]{1,0:T(8,128)S(1)} %get-tuple-element.228) | copy-start | bytes 50331652 | tf_op jit(solution)/shard_map/cond/branch_1_fun/while
  255.8 6.2 %copy-start = (f32[512,8192]{1,0:T(8,128)}, f32[512,8192]{1,0:T(8,128)S(1)}, u32[]{:S(2)}) copy-start(f32[512,8192]{1,0:T(8,128)S(1)} %get-tuple-element.228) | copy-start | bytes 50331652 | tf_op jit(solution)/shard_map/cond/branch_1_fun/while
  282.7 6.2 %copy-start = (f32[512,8192]{1,0:T(8,128)}, f32[512,8192]{1,0:T(8,128)S(1)}, u32[]{:S(2)}) copy-start(f32[512,8192]{1,0:T(8,128)S(1)} %get-tuple-element.228) | copy-start | bytes 50331652 | tf_op jit(solution)/shard_map/cond/branch_1_fun/while
  309.7 6.2 %copy-start = (f32[512,8192]{1,0:T(8,128)}, f32[512,8192]{1,0:T(8,128)S(1)}, u32[]{:S(2)}) copy-start(f32[512,8192]{1,0:T(8,128)S(1)} %get-tuple-element.228) | copy-start | bytes 50331652 | tf_op jit(solution)/shard_map/cond/branch_1_fun/while
  336.7 6.2 %copy-start = (f32[512,8192]{1,0:T(8,128)}, f32[512,8192]{1,0:T(8,128)S(1)}, u32[]{:S(2)}) copy-start(f32[512,8192]{1,0:T(8,128)S(1)} %get-tuple-element.228) | copy-start | bytes 50331652 | tf_op jit(solution)/shard_map/cond/branch_1_fun/while
Sparse Core Ops, SparseCore 0:
  30.3 37.7 all-gather.1
where the time goes:
time: 408 us; the launch traced here: 407 us
  matrix products  127 us (31%)
  other arithmetic  106 us (26%)
  local copies, waits for them, and re-layouts  62.7 us (15%)
  blocking collectives  50.7 us (12%)
  waiting for transfers between devices  24.6 us (6%)
  loops' own time  17.2 us (4%)
  between operations  14.8 us (4%)
    dot_general x8, matrix products, one_head(): jnp.dot(expo.astype(jnp.bfloat16), vh, preferred_element_type=jnp.float32)  72.5 us
    dot_general x8, matrix products, one_head(): scores = jnp.dot(qh, kh.T, preferred_element_type=jnp.float32) * scale  54.3 us
    unnamed x2, other arithmetic  51.8 us
    reduce_sum x8, other arithmetic, one_head(): summed = summed * factor + jnp.sum(expo, axis=1)  49.4 us
    all_to_all x1, blocking collectives, on_device(): lax.all_to_all(outputs, 'uly', split_axis=1, concat_axis=2, tiled=True)  31.7 us
    all_to_all x1, waiting for transfers between devices, on_device(): lax.all_to_all(queries, 'uly', split_axis=2, concat_axis=1, tiled=True)  24.5 us
    unnamed x13, local copies, waits for them, and re-layouts  20.5 us
    all_to_all x1, blocking collectives, side_by_side(): lax.all_to_all(both, axis, split_axis=split_dim, concat_axis=concat_dim,...  19.1 us
  transfers between devices with their start and end apart: 2, of which 1 were waited for; matrix products, arithmetic and copies ran while one was open for 18% of the time, Pallas kernels for 0%

commit v1 on v0

--- a/solution.py
+++ b/solution.py
@@ -28,7 +28,12 @@
 
 def on_device(queries, keys, values, doc_blocks):
     moved_q, moved_k, moved_v = (
-        lax.all_to_all(queries, "uly", split_axis=2, concat_axis=1, tiled=True),
+        jnp.concatenate(
+            lax.all_to_all(
+                jnp.stack(jnp.split(queries, lax.axis_size("uly"), axis=2)), "uly", 0, 0
+            ),
+            axis=1,
+        ),
         *side_by_side((keys, values), "uly", 2, 1, 0),
     )
     slot = moved_q.shape[1]

time: 408 us -> 411 us (level)
  the two profiles are of different devices: /device:TPU:720 before, /device:TPU:513 now
where the time goes in v1:
time: 411 us; the launch traced here: 410 us
  matrix products  127 us (31%)
  local copies, waits for them, and re-layouts  96 us (23%)
  other arithmetic  60.8 us (15%)
  blocking collectives  51.3 us (12%)
  waiting for transfers between devices  39.4 us (10%)
  loops' own time  16.9 us (4%)
  between operations  14.8 us (4%)
    dot_general x8, matrix products, one_head(): jnp.dot(expo.astype(jnp.bfloat16), vh, preferred_element_type=jnp.float32)  72.5 us
    dot_general x8, matrix products, one_head(): scores = jnp.dot(qh, kh.T, preferred_element_type=jnp.float32) * scale  54.2 us
    reduce_sum x8, other arithmetic, one_head(): summed = summed * factor + jnp.sum(expo, axis=1)  49.2 us
    while x16, local copies, waits for them, and re-layouts  45.6 us
    all_to_all x1, blocking collectives, on_device(): lax.all_to_all(outputs, 'uly', split_axis=1, concat_axis=2, tiled=True)  34.3 us
    all_gather x1, waiting for transfers between devices, on_device(): piece = lax.all_gather(stacked, 'blk', axis=1, tiled=True)  26.5 us
    dynamic_update_slice x24, local copies, waits for them, and re-layouts, work(): lax.map(one_head, (jnp.arange(local_q, dtype=jnp.int32),) + tuple(state))  17.5 us
    all_to_all x1, blocking collectives, side_by_side(): lax.all_to_all(both, axis, split_axis=split_dim, concat_axis=concat_dim,...  17 us
  transfers between devices with their start and end apart: 2, of which 2 were waited for; matrix products, arithmetic and copies ran while one was open for 4% of the time, Pallas kernels for 0%

profile of v1, /device:TPU:513, one launch (start us, length us, event | category | flops | bytes accessed | tf_op | source)
XLA Modules:
  0.0 409.7 jit_solution(16165551560217072339)
XLA Ops:
  8.3 17.0 %all_to_all.38 = bf16[8,2,8192]{2,1,0:T(2,128)(2,1)S(1)} all-to-all(bf16[8,2,8192]{2,1,0:T(2,128)(2,1)S(1)} %reshape.77), channel_id=1, replica_groups=mesh['parts'=2,'uly'=8,'blk'=16] {'uly'}, dimensions={0} | all-to-all | bytes 524288 | tf_op jit(solution)/shard_map/all_to_all | solution.py:18
  47.8 12.9 %all-to-all-done.1 = bf16[8,1,64,1024]{3,2,1,0:T(8,128)(2,1)S(1)} async-done(((bf16[8,1,64,1024]{3,2,1,0:T(8,128)(2,1)}), bf16[8,1,64,1024]{3,2,1,0:T(8,128)(2,1)S(1)}, u32[]{:S(2)}, u32[]{:S(2)}) %all-to-all-start.1) | async-done | bytes 1048608 | tf_op jit(solution)/shard_map/all_to_all | solution.py:32
  61.0 26.5 %all-gather.2.cloned.1.call-done = bf16[2,8192,128]{2,1,0:T(8,128)(2,1)} async-done(((bf16[2,512,128]{2,1,0:T(8,128)(2,1)}), bf16[2,8192,128]{2,1,0:T(8,128)(2,1)}) %all-gather.2.cloned.1.call-update) | async-done | bytes 4194320 | tf_op jit(solution)/shard_map/all_gather | solution.py:60
  87.5 266.6 %conditional.1 = (f32[8,512]{1,0:T(8,128)}, f32[8,512,128]{1,2,0:T(8,128)}) conditional(s32[]{:T(128)} %convert_element_type.20, () %tuple.17, (bf16[2,8192,128]{2,1,0:T(8,128)(2,1)}, s32[512]{0:T(512)S(1)}, s32[16]{0:T(128)S(1)}, s32[]{:T(128)}, s32[512]{0:T(512)S(1)}, /*index=5*/bf16[8,512,128]{2,0,1:T(8,128)(2,1)S(1)}) %tuple.52), branch_computations={%region_3.4_spmd, %region_4.10_spmd} | conditional | flops 2240210944 | bytes 133736896 | solution.py:89
  92.6 261.4 %while.12 = (s32[]{:T(128)}, f32[8,512]{1,0:T(8,128)}, f32[8,512,128]{1,2,0:T(8,128)}, s32[8]{0:T(128)S(1)}, bf16[8,512,128]{2,1,0:T(8,128)(2,1)}, /*index=5*/bf...) while((s32[]{:T(128)}, f32[8,512]{1,0:T(8,128)}, ...), condition=%wide.region_9.9_spmd.clone, body=%wide.region_6.8_spmd.clone.sunk | while | flops 2239825408 | bytes 123214048 | solution.py:85
  95.4 6.8 %fusion.37 = (f32[512]{0:T(512)S(1)}, f32[512,8192]{1,0:T(8,128)S(1)}) fusion(s32[512]{0:T(512)S(1)} %get-tuple-element.260, s32[8192]{0:T(1024)S(1)} %get-tuple-element.258, s32[512]{0:T(512)S(1)} %get-tuple-element.259, bf16[8192,1,128]{2,0,1:T(8,128)(2,1)} %get-tuple-element.256, bf16[8,512,128]{2,1,0:T(8,128)(2,1)} %get-tuple-element.255, ...), kind=kOutput, calls=%fused_computation.5.clone.1 | convolution fusion | flops 1098907136 | bytes 19044356 | tf_op jit(solution)/shard_map/cond/branch_1_fun/while/body/eval_jaxpr/dot_general | solution.py:74
  115.4 9.1 %fusion.39 = f32[1,512,128]{2,1,0:T(8,128)S(1)} fusion(bf16[8192,1,128]{2,0,1:T(8,128)(2,1)S(1)} %get-tuple-element.257, f32[512,8192]{1,0:T(8,128)} %copy-done, s32[512]{0:T(512)S(1)} %get-tuple-element.260, s32[8192]{0:T(1024)S(1)} %get-tuple-element.258, f32[512]{0:T(512)S(1)} %broadcast_maximum_fusion.2, s32[512]{0:T(512)S(1)} %get-tuple-element.259, ...), kind=kOutput, calls=%fused_computation.13.clone.1 | convolution fusion | flops 1107361792 | bytes 19177472 | tf_op jit(solution)/shard_map/cond/branch_1_fun/while/body/eval_jaxpr/dot_general | solution.py:80
  128.0 6.8 %fusion.37 = (f32[512]{0:T(512)S(1)}, f32[512,8192]{1,0:T(8,128)S(1)}) fusion(s32[512]{0:T(512)S(1)} %get-tuple-element.260, s32[8192]{0:T(1024)S(1)} %get-tuple-element.258, s32[512]{0:T(512)S(1)} %get-tuple-element.259, bf16[8192,1,128]{2,0,1:T(8,128)(2,1)} %get-tuple-element.256, bf16[8,512,128]{2,1,0:T(8,128)(2,1)} %get-tuple-element.255, ...), kind=kOutput, calls=%fused_computation.5.clone.1 | convolution fusion | flops 1098907136 | bytes 19044356 | tf_op jit(solution)/shard_map/cond/branch_1_fun/while/body/eval_jaxpr/dot_general | solution.py:74
  148.0 9.1 %fusion.39 = f32[1,512,128]{2,1,0:T(8,128)S(1)} fusion(bf16[8192,1,128]{2,0,1:T(8,128)(2,1)S(1)} %get-tuple-element.257, f32[512,8192]{1,0:T(8,128)} %copy-done, s32[512]{0:T(512)S(1)} %get-tuple-element.260, s32[8192]{0:T(1024)S(1)} %get-tuple-element.258, f32[512]{0:T(512)S(1)} %broadcast_maximum_fusion.2, s32[512]{0:T(512)S(1)} %get-tuple-element.259, ...), kind=kOutput, calls=%fused_computation.13.clone.1 | convolution fusion | flops 1107361792 | bytes 19177472 | tf_op jit(solution)/shard_map/cond/branch_1_fun/while/body/eval_jaxpr/dot_general | solution.py:80
  160.7 6.8 %fusion.37 = (f32[512]{0:T(512)S(1)}, f32[512,8192]{1,0:T(8,128)S(1)}) fusion(s32[512]{0:T(512)S(1)} %get-tuple-element.260, s32[8192]{0:T(1024)S(1)} %get-tuple-element.258, s32[512]{0:T(512)S(1)} %get-tuple-element.259, bf16[8192,1,128]{2,0,1:T(8,128)(2,1)} %get-tuple-element.256, bf16[8,512,128]{2,1,0:T(8,128)(2,1)} %get-tuple-element.255, ...), kind=kOutput, calls=%fused_computation.5.clone.1 | convolution fusion | flops 1098907136 | bytes 19044356 | tf_op jit(solution)/shard_map/cond/branch_1_fun/while/body/eval_jaxpr/dot_general | solution.py:74
  180.7 9.1 %fusion.39 = f32[1,512,128]{2,1,0:T(8,128)S(1)} fusion(bf16[8192,1,128]{2,0,1:T(8,128)(2,1)S(1)} %get-tuple-element.257, f32[512,8192]{1,0:T(8,128)} %copy-done, s32[512]{0:T(512)S(1)} %get-tuple-element.260, s32[8192]{0:T(1024)S(1)} %get-tuple-element.258, f32[512]{0:T(512)S(1)} %broadcast_maximum_fusion.2, s32[512]{0:T(512)S(1)} %get-tuple-element.259, ...), kind=kOutput, calls=%fused_computation.13.clone.1 | convolution fusion | flops 1107361792 | bytes 19177472 | tf_op jit(solution)/shard_map/cond/branch_1_fun/while/body/eval_jaxpr/dot_general | solution.py:80
  193.4 6.8 %fusion.37 = (f32[512]{0:T(512)S(1)}, f32[512,8192]{1,0:T(8,128)S(1)}) fusion(s32[512]{0:T(512)S(1)} %get-tuple-element.260, s32[8192]{0:T(1024)S(1)} %get-tuple-element.258, s32[512]{0:T(512)S(1)} %get-tuple-element.259, bf16[8192,1,128]{2,0,1:T(8,128)(2,1)} %get-tuple-element.256, bf16[8,512,128]{2,1,0:T(8,128)(2,1)} %get-tuple-element.255, ...), kind=kOutput, calls=%fused_computation.5.clone.1 | convolution fusion | flops 1098907136 | bytes 19044356 | tf_op jit(solution)/shard_map/cond/branch_1_fun/while/body/eval_jaxpr/dot_general | solution.py:74
  205.9 6.2 %fusion.38 = f32[512]{0:T(512)S(1)} fusion(f32[512,8192]{1,0:T(8,128)S(1)} %get-tuple-element.222, s32[512]{0:T(512)S(1)} %get-tuple-element.260, s32[8192]{0:T(1024)S(1)} %get-tuple-element.258, f32[512]{0:T(512)S(1)} %broadcast_maximum_fusion.2, s32[512]{0:T(512)S(1)} %get-tuple-element.259), kind=kLoop, calls=%fused_computation.7.clone.1 | loop fusion | flops 33553920 | bytes 16818176 | tf_op jit(solution)/shard_map/cond/branch_1_fun/while/body/eval_jaxpr/reduce_sum | solution.py:79
  213.4 9.1 %fusion.39 = f32[1,512,128]{2,1,0:T(8,128)S(1)} fusion(bf16[8192,1,128]{2,0,1:T(8,128)(2,1)S(1)} %get-tuple-element.257, f32[512,8192]{1,0:T(8,128)} %copy-done, s32[512]{0:T(512)S(1)} %get-tuple-element.260, s32[8192]{0:T(1024)S(1)} %get-tuple-element.258, f32[512]{0:T(512)S(1)} %broadcast_maximum_fusion.2, s32[512]{0:T(512)S(1)} %get-tuple-element.259, ...), kind=kOutput, calls=%fused_computation.13.clone.1 | convolution fusion | flops 1107361792 | bytes 19177472 | tf_op jit(solution)/shard_map/cond/branch_1_fun/while/body/eval_jaxpr/dot_general | solution.py:80
  226.1 6.8 %fusion.37 = (f32[512]{0:T(512)S(1)}, f32[512,8192]{1,0:T(8,128)S(1)}) fusion(s32[512]{0:T(512)S(1)} %get-tuple-element.260, s32[8192]{0:T(1024)S(1)} %get-tuple-element.258, s32[512]{0:T(512)S(1)} %get-tuple-element.259, bf16[8192,1,128]{2,0,1:T(8,128)(2,1)} %get-tuple-element.256, bf16[8,512,128]{2,1,0:T(8,128)(2,1)} %get-tuple-element.255, ...), kind=kOutput, calls=%fused_computation.5.clone.1 | convolution fusion | flops 1098907136 | bytes 19044356 | tf_op jit(solution)/shard_map/cond/branch_1_fun/while/body/eval_jaxpr/dot_general | solution.py:74
  246.1 9.1 %fusion.39 = f32[1,512,128]{2,1,0:T(8,128)S(1)} fusion(bf16[8192,1,128]{2,0,1:T(8,128)(2,1)S(1)} %get-tuple-element.257, f32[512,8192]{1,0:T(8,128)} %copy-done, s32[512]{0:T(512)S(1)} %get-tuple-element.260, s32[8192]{0:T(1024)S(1)} %get-tuple-element.258, f32[512]{0:T(512)S(1)} %broadcast_maximum_fusion.2, s32[512]{0:T(512)S(1)} %get-tuple-element.259, ...), kind=kOutput, calls=%fused_computation.13.clone.1 | convolution fusion | flops 1107361792 | bytes 19177472 | tf_op jit(solution)/shard_map/cond/branch_1_fun/while/body/eval_jaxpr/dot_general | solution.py:80
  258.7 6.8 %fusion.37 = (f32[512]{0:T(512)S(1)}, f32[512,8192]{1,0:T(8,128)S(1)}) fusion(s32[512]{0:T(512)S(1)} %get-tuple-element.260, s32[8192]{0:T(1024)S(1)} %get-tuple-element.258, s32[512]{0:T(512)S(1)} %get-tuple-element.259, bf16[8192,1,128]{2,0,1:T(8,128)(2,1)} %get-tuple-element.256, bf16[8,512,128]{2,1,0:T(8,128)(2,1)} %get-tuple-element.255, ...), kind=kOutput, calls=%fused_computation.5.clone.1 | convolution fusion | flops 1098907136 | bytes 19044356 | tf_op jit(solution)/shard_map/cond/branch_1_fun/while/body/eval_jaxpr/dot_general | solution.py:74
  278.7 9.1 %fusion.39 = f32[1,512,128]{2,1,0:T(8,128)S(1)} fusion(bf16[8192,1,128]{2,0,1:T(8,128)(2,1)S(1)} %get-tuple-element.257, f32[512,8192]{1,0:T(8,128)} %copy-done, s32[512]{0:T(512)S(1)} %get-tuple-element.260, s32[8192]{0:T(1024)S(1)} %get-tuple-element.258, f32[512]{0:T(512)S(1)} %broadcast_maximum_fusion.2, s32[512]{0:T(512)S(1)} %get-tuple-element.259, ...), kind=kOutput, calls=%fused_computation.13.clone.1 | convolution fusion | flops 1107361792 | bytes 19177472 | tf_op jit(solution)/shard_map/cond/branch_1_fun/while/body/eval_jaxpr/dot_general | solution.py:80
  291.4 6.8 %fusion.37 = (f32[512]{0:T(512)S(1)}, f32[512,8192]{1,0:T(8,128)S(1)}) fusion(s32[512]{0:T(512)S(1)} %get-tuple-element.260, s32[8192]{0:T(1024)S(1)} %get-tuple-element.258, s32[512]{0:T(512)S(1)} %get-tuple-element.259, bf16[8192,1,128]{2,0,1:T(8,128)(2,1)} %get-tuple-element.256, bf16[8,512,128]{2,1,0:T(8,128)(2,1)} %get-tuple-element.255, ...), kind=kOutput, calls=%fused_computation.5.clone.1 | convolution fusion | flops 1098907136 | bytes 19044356 | tf_op jit(solution)/shard_map/cond/branch_1_fun/while/body/eval_jaxpr/dot_general | solution.py:74
  311.4 9.1 %fusion.39 = f32[1,512,128]{2,1,0:T(8,128)S(1)} fusion(bf16[8192,1,128]{2,0,1:T(8,128)(2,1)S(1)} %get-tuple-element.257, f32[512,8192]{1,0:T(8,128)} %copy-done, s32[512]{0:T(512)S(1)} %get-tuple-element.260, s32[8192]{0:T(1024)S(1)} %get-tuple-element.258, f32[512]{0:T(512)S(1)} %broadcast_maximum_fusion.2, s32[512]{0:T(512)S(1)} %get-tuple-element.259, ...), kind=kOutput, calls=%fused_computation.13.clone.1 | convolution fusion | flops 1107361792 | bytes 19177472 | tf_op jit(solution)/shard_map/cond/branch_1_fun/while/body/eval_jaxpr/dot_general | solution.py:80
  324.1 6.8 %fusion.37 = (f32[512]{0:T(512)S(1)}, f32[512,8192]{1,0:T(8,128)S(1)}) fusion(s32[512]{0:T(512)S(1)} %get-tuple-element.260, s32[8192]{0:T(1024)S(1)} %get-tuple-element.258, s32[512]{0:T(512)S(1)} %get-tuple-element.259, bf16[8192,1,128]{2,0,1:T(8,128)(2,1)} %get-tuple-element.256, bf16[8,512,128]{2,1,0:T(8,128)(2,1)} %get-tuple-element.255, ...), kind=kOutput, calls=%fused_computation.5.clone.1 | convolution fusion | flops 1098907136 | bytes 19044356 | tf_op jit(solution)/shard_map/cond/branch_1_fun/while/body/eval_jaxpr/dot_general | solution.py:74
  344.1 9.1 %fusion.39 = f32[1,512,128]{2,1,0:T(8,128)S(1)} fusion(bf16[8192,1,128]{2,0,1:T(8,128)(2,1)S(1)} %get-tuple-element.257, f32[512,8192]{1,0:T(8,128)} %copy-done, s32[512]{0:T(512)S(1)} %get-tuple-element.260, s32[8192]{0:T(1024)S(1)} %get-tuple-element.258, f32[512]{0:T(512)S(1)} %broadcast_maximum_fusion.2, s32[512]{0:T(512)S(1)} %get-tuple-element.259, ...), kind=kOutput, calls=%fused_computation.13.clone.1 | convolution fusion | flops 1107361792 | bytes 19177472 | tf_op jit(solution)/shard_map/cond/branch_1_fun/while/body/eval_jaxpr/dot_general | solution.py:80
  358.4 6.8 %reduce.2 = bf16[512,1024]{1,0:T(8,128)(2,1)S(1)} reduce(bf16[512,1,1024]{2,1,0:T(2,128)(2,1)S(1)} %bitcast.79, bf16[]{:T(256)} %broadcast.102), dimensions={1}, to_apply=%bitcast.60.reduce_sub_computation | reduce | bytes 2097154
  366.0 34.3 %all_to_all.39 = bf16[8,2,32768]{2,1,0:T(2,128)(2,1)S(1)} all-to-all(bf16[8,2,32768]{2,1,0:T(2,128)(2,1)S(1)} %reshape.79), channel_id=1, replica_groups=mesh['parts'=2,'uly'=8,'blk'=16] {'uly'}, dimensions={0} | all-to-all | bytes 2097152 | tf_op jit(solution)/shard_map/all_to_all | solution.py:92
  (113 shorter events, 147.7 us)
Async XLA Ops:
  6.5 80.9 %all-gather.2.cloned.1.call-start = ((), (), s32[]{:S(2)}) async-start(), calls=%async_computation.3 | async-start | bytes 4456448 | tf_op jit(solution)/shard_map/all_gather | solution.py:60
  40.6 20.1 %all-to-all-start.1 = ((bf16[8,1,64,1024]{3,2,1,0:T(8,128)(2,1)}), bf16[8,1,64,1024]{3,2,1,0:T(8,128)(2,1)S(1)}, u32[]{:S(2)}, u32[]{:S(2)}) async-start(bf16[8,1,64,1024]{3,2,1,0:T(8,128)(2,1)} %bitcast_dynamic-update-slice_fusion), calls=%async_computation.1 | async-start | bytes 2097152 | tf_op jit(solution)/shard_map/all_to_all | solution.py:32
  102.2 5.7 %copy-start = (f32[512,8192]{1,0:T(8,128)}, f32[512,8192]{1,0:T(8,128)S(1)}, u32[]{:S(2)}) copy-start(f32[512,8192]{1,0:T(8,128)S(1)} %get-tuple-element.222) | copy-start | bytes 50331652 | tf_op jit(solution)/shard_map/cond/branch_1_fun/while
  134.8 5.7 %copy-start = (f32[512,8192]{1,0:T(8,128)}, f32[512,8192]{1,0:T(8,128)S(1)}, u32[]{:S(2)}) copy-start(f32[512,8192]{1,0:T(8,128)S(1)} %get-tuple-element.222) | copy-start | bytes 50331652 | tf_op jit(solution)/shard_map/cond/branch_1_fun/while
  167.5 5.7 %copy-start = (f32[512,8192]{1,0:T(8,128)}, f32[512,8192]{1,0:T(8,128)S(1)}, u32[]{:S(2)}) copy-start(f32[512,8192]{1,0:T(8,128)S(1)} %get-tuple-element.222) | copy-start | bytes 50331652 | tf_op jit(solution)/shard_map/cond/branch_1_fun/while
  200.2 5.7 %copy-start = (f32[512,8192]{1,0:T(8,128)}, f32[512,8192]{1,0:T(8,128)S(1)}, u32[]{:S(2)}) copy-start(f32[512,8192]{1,0:T(8,128)S(1)} %get-tuple-element.222) | copy-start | bytes 50331652 | tf_op jit(solution)/shard_map/cond/branch_1_fun/while
  232.8 5.7 %copy-start = (f32[512,8192]{1,0:T(8,128)}, f32[512,8192]{1,0:T(8,128)S(1)}, u32[]{:S(2)}) copy-start(f32[512,8192]{1,0:T(8,128)S(1)} %get-tuple-element.222) | copy-start | bytes 50331652 | tf_op jit(solution)/shard_map/cond/branch_1_fun/while
  265.5 5.7 %copy-start = (f32[512,8192]{1,0:T(8,128)}, f32[512,8192]{1,0:T(8,128)S(1)}, u32[]{:S(2)}) copy-start(f32[512,8192]{1,0:T(8,128)S(1)} %get-tuple-element.222) | copy-start | bytes 50331652 | tf_op jit(solution)/shard_map/cond/branch_1_fun/while
  298.2 5.7 %copy-start = (f32[512,8192]{1,0:T(8,128)}, f32[512,8192]{1,0:T(8,128)S(1)}, u32[]{:S(2)}) copy-start(f32[512,8192]{1,0:T(8,128)S(1)} %get-tuple-element.222) | copy-start | bytes 50331652 | tf_op jit(solution)/shard_map/cond/branch_1_fun/while
  330.8 5.7 %copy-start = (f32[512,8192]{1,0:T(8,128)}, f32[512,8192]{1,0:T(8,128)S(1)}, u32[]{:S(2)}) copy-start(f32[512,8192]{1,0:T(8,128)S(1)} %get-tuple-element.222) | copy-start | bytes 50331652 | tf_op jit(solution)/shard_map/cond/branch_1_fun/while
Sparse Core Ops, SparseCore 0:
  28.2 59.1 all-gather.1
